TPU v7x, 32 devices: a whole 2x2x4 slice. The times are simulated.
32 devices in a mesh: depth: 4 (over y, core), blk: 8 (over z, x).
Axes of the slice: x: 2, y: 2, z: 4, core: 2. Of those that a mesh axis runs over, the one named last changes fastest.
Arguments:
- jacobian: bfloat16 [96, 16384], P(('depth', 'blk')), may hold values from -6 to 6
- gain_inverse: bfloat16 [16384, 16384], P('depth', 'blk'), may hold values from -0.00024414062 to 0.00048828125, as said below
- variance: float32 [96], P(('depth', 'blk')), may hold values from 2 to 12
Outputs:
- omega_diag: float32 [96], P(('depth', 'blk'))
Inputs may be any that keep to these rules, and one draw needn't show every extreme that they name: gain_inverse is symmetric and positive definite.
All inputs are finite; a program needn't handle non-finite values.
Results may differ from a plain program's by a relative error of at most 0.0003.
Values may be sent and summed in bfloat16 or wider, within the bound.
A program may use at most 128 MiB of HBM per device.

v0:
```python
import jax
import jax.numpy as jnp
from jax import lax
from jax.sharding import PartitionSpec as P


def shards(jacobian, gain_inverse, variance):
    rows_local = jacobian.shape[0]
    depth_count = lax.axis_size("depth")
    blk_count = lax.axis_size("blk")
    quarter_rows = lax.all_to_all(jacobian, "depth", split_axis=1, concat_axis=0, tiled=True)
    whole_rows = lax.all_gather(jacobian, "depth", axis=0, tiled=True)
    panel = lax.all_to_all(whole_rows, "blk", split_axis=1, concat_axis=0, tiled=True)
    projected = jnp.dot(
        lax.all_gather(quarter_rows, "blk", axis=0, tiled=True),
        gain_inverse,
        preferred_element_type=jnp.float32,
    )
    partial_sum = jnp.sum(projected * panel.astype(jnp.float32), axis=1)
    by_section = partial_sum.reshape(blk_count, depth_count * rows_local)
    reduced = lax.psum_scatter(by_section, "blk", scatter_dimension=0, tiled=True).reshape(-1)
    quadratic = lax.psum_scatter(reduced, "depth", scatter_dimension=0, tiled=True)
    return variance - quadratic


def solution(mesh):
    in_specs = (P(("depth", "blk"), None), P("depth", "blk"), P(("depth", "blk")))
    out_specs = P(("depth", "blk"))
    return jax.shard_map(shards, mesh=mesh, in_specs=in_specs, out_specs=out_specs, check_vma=False)
```

profile of v0, /device:TPU:0, one launch (start us, length us, event | category | flops | bytes accessed | tf_op | source)
XLA Modules:
  0.0 96.0 jit_solution(18339546582499330617)
XLA Ops:
  0.0 4.3 %all-to-all-start = ((bf16[3,4,4096]{2,0,1:T(4,128)(2,1)}), bf16[3,4,4096]{2,0,1:T(4,128)(2,1)S(1)}, u32[]{:S(2)}, u32[]{:S(2)}) async-start(bf16[3,4,4096]{2,0,1:T(4,128)(2,1)} %bitcast.11), calls=%async_computation | async-start | bytes 262144 | tf_op jit(solution)/shard_map/all_to_all | solution.py:11
  4.3 8.3 %all-gather.1 = bf16[4,3,16384]{2,1,0:T(4,128)(2,1)S(1)} all-gather(bf16[1,3,16384]{2,1,0:T(4,128)(2,1)} %bitcast.12), channel_id=1, replica_groups=mesh['depth'=4,'blk'=8] {'depth'}, dimensions={0}, use_global_device_ids=true | all-gather | bytes 491520 | tf_op jit(solution)/shard_map/all_gather | solution.py:12
  12.5 0.5 all_to_all.28
  13.1 0.0 copy-start
  13.1 1.0 %copy.8 = bf16[12,8,2048]{2,0,1:T(8,128)(2,1)} copy(bf16[12,8,2048]{2,1,0:T(8,128)(2,1)S(1)} %all_to_all.28) | data formatting | bytes 786432 | tf_op jit(solution)/shard_map/all_to_all | solution.py:13
  14.1 0.0 all-to-all-done
  14.1 6.3 %all-to-all-start.1 = ((bf16[12,8,2048]{2,0,1:T(8,128)(2,1)}), bf16[12,8,2048]{2,0,1:T(8,128)(2,1)S(1)}, u32[]{:S(2)}, u32[]{:S(2)}) async-start(bf16[12,8,2048]{2,0,1:T(8,128)(2,1)} %copy.8), calls=%async_computation.1 | async-start | bytes 1048576 | tf_op jit(solution)/shard_map/all_to_all | solution.py:13
  20.4 1.2 %dynamic-slice = u32[1]{0:T(128)} dynamic-slice(u32[32]{0:T(128)} %constant.6, u32[]{:T(128)S(6)} %add.5), dynamic_slice_sizes={1} | dynamic-slice | bytes 12
  21.7 1.3 %dynamic-slice.2 = u32[1]{0:T(128)} dynamic-slice(u32[32]{0:T(128)} %constant.10, u32[]{:T(128)S(6)} %add.5), dynamic_slice_sizes={1} | dynamic-slice | bytes 12
  23.0 0.1 reshape.17
  23.1 37.9 %all-gather = bf16[8,12,4096]{2,1,0:T(8,128)(2,1)S(1)} all-gather(bf16[1,12,4096]{2,1,0:T(8,128)(2,1)S(1)} %reshape.17), channel_id=1, replica_groups=mesh['depth'=4,'blk'=8] {'blk'}, dimensions={0}, use_global_device_ids=true | all-gather | bytes 884736 | tf_op jit(solution)/shard_map/all_gather | solution.py:15
  61.0 0.2 reshape.18
  61.1 0.0 all-to-all-done.1
  61.2 0.1 convert_bitcast_fusion
  61.3 0.1 reshape.16
  61.4 8.7 %fusion = f32[96]{0:T(128)S(1)} fusion(f32[96,2048]{1,0:T(8,128)S(1)} %reshape.16, bf16[96,4096]{1,0:T(8,128)(2,1)S(1)} %reshape.18, bf16[4096,2048]{1,0:T(8,128)(2,1)} %param.4), kind=kOutput, calls=%fused_computation.1 | convolution fusion | flops 1611005824 | bytes 18350464 | tf_op jit(solution)/shard_map/dot_general | solution.py:14
  70.0 0.1 reshape.14
  70.1 18.3 %all-reduce = f32[8,12]{1,0:T(8,128)S(1)} all-reduce(f32[8,12]{1,0:T(8,128)S(1)} %reshape.14), channel_id=2, replica_groups=mesh['depth'=4,'blk'=8] {'blk'}, use_global_device_ids=true, to_apply=%region_1.0.clone | all-reduce | flops 96 | bytes 768
  88.4 0.6 dynamic-slice_bitcast_fusion
  89.7 5.7 %all-reduce.1 = f32[12]{0:T(128)S(1)} all-reduce(f32[12]{0:T(128)S(1)} %dynamic-slice_bitcast_fusion), channel_id=3, replica_groups=mesh['depth'=4,'blk'=8] {'depth'}, use_global_device_ids=true, to_apply=%region_2.0.clone | all-reduce | flops 12 | bytes 96
  95.4 0.0 copy-done
  95.4 0.6 dynamic-slice_subtract_fusion
Async XLA Ops:
  0.0 14.1 %all-to-all-start = ((bf16[3,4,4096]{2,0,1:T(4,128)(2,1)}), bf16[3,4,4096]{2,0,1:T(4,128)(2,1)S(1)}, u32[]{:S(2)}, u32[]{:S(2)}) async-start(bf16[3,4,4096]{2,0,1:T(4,128)(2,1)} %bitcast.11), calls=%async_computation | async-start | bytes 262144 | tf_op jit(solution)/shard_map/all_to_all | solution.py:11
  13.1 82.3 %copy-start = (f32[3]{0:T(128)S(1)}, f32[3]{0:T(128)}, u32[]{:S(2)}) copy-start(f32[3]{0:T(128)} %param.5) | copy-start | bytes 40
  14.1 47.0 %all-to-all-start.1 = ((bf16[12,8,2048]{2,0,1:T(8,128)(2,1)}), bf16[12,8,2048]{2,0,1:T(8,128)(2,1)S(1)}, u32[]{:S(2)}, u32[]{:S(2)}) async-start(bf16[12,8,2048]{2,0,1:T(8,128)(2,1)} %copy.8), calls=%async_computation.1 | async-start | bytes 1048576 | tf_op jit(solution)/shard_map/all_to_all | solution.py:13
where the time goes:
time: 96.4 us; the launch traced here: 96 us
  blocking collectives  70.1 us (73%)
  starting transfers between devices  10.6 us (11%)
  matrix products  8.66 us (9%)
  local copies, waits for them, and re-layouts  5.19 us (5%)
    all_gather x1, blocking collectives, shards(): lax.all_gather(quarter_rows, 'blk', axis=0, tiled=True)  37.9 us
    unnamed x2, blocking collectives  24 us
    dot_general x1, matrix products, shards(): jnp.dot(lax.all_gather(quarter_rows, 'blk', axis=0, tiled=True), gain_inv...  8.66 us
    all_gather x1, blocking collectives, shards(): whole_rows = lax.all_gather(jacobian, 'depth', axis=0, tiled=True)  8.27 us
    all_to_all x1, starting transfers between devices, shards(): lax.all_to_all(whole_rows, 'blk', split_axis=1, concat_axis=0, tiled=True)  6.31 us
    all_to_all x1, starting transfers between devices, shards(): lax.all_to_all(jacobian, 'depth', split_axis=1, concat_axis=0, tiled=True)  4.26 us
    unnamed x6, local copies, waits for them, and re-layouts  2.82 us
  transfers between devices with their start and end apart: 2, of which 0 were waited for; matrix products, arithmetic and copies ran while one was open for 4% of the time, Pallas kernels for 0%

commit v1 on v0

v1 whole, which is shorter than its diff:
```python
import functools

import jax
import jax.numpy as jnp
from jax import lax
from jax.experimental import pallas as pl
from jax.experimental.pallas import tpu as pltpu
from jax.sharding import PartitionSpec as P

LANES = 128
SUBLANES = 8
MESH = pl.DeviceIdType.MESH


def exchange_kernel(depth_count, blk_count, slots, *refs):
    count = len(slots)
    sources, targets = refs[:count], refs[count : 2 * count]
    send_sem, recv_sem, own_sem = refs[2 * count :]
    devices = depth_count * blk_count
    me = lax.axis_index("depth") * blk_count + lax.axis_index("blk")

    def place(device):
        return {"depth": device // blk_count, "blk": lax.rem(device, blk_count)}

    def peer(step):
        return lax.rem(me + step, devices)

    def slot_of(kind, device):
        if kind == "depth":
            return device // blk_count
        if kind == "blk":
            return lax.rem(device, blk_count)
        return device

    def copy(which, step):
        device = peer(step)
        return pltpu.make_async_remote_copy(
            src_ref=sources[which].at[slot_of(slots[which], device)],
            dst_ref=targets[which].at[me],
            send_sem=send_sem.at[which, step],
            recv_sem=recv_sem.at[which, step],
            device_id=place(device),
            device_id_type=MESH,
        )

    barrier = pltpu.get_barrier_semaphore()

    @pl.loop(1, devices)
    def _(step):
        pl.semaphore_signal(barrier, inc=1, device_id=place(peer(step)), device_id_type=MESH)

    own = [
        pltpu.make_async_copy(sources[w].at[slot_of(slots[w], me)], targets[w].at[me], own_sem.at[w])
        for w in range(count)
    ]
    for w in range(count):
        own[w].start()
    pl.semaphore_wait(barrier, devices - 1)

    @pl.loop(1, devices)
    def _(step):
        for w in range(count):
            copy(w, step).start()

    for w in range(count):
        own[w].wait()

    @pl.loop(1, devices)
    def _(step):
        for w in range(count):
            copy(w, step).wait()


def exchange(slots, collective_id, *operands):
    depth_count = lax.axis_size("depth")
    blk_count = lax.axis_size("blk")
    devices = depth_count * blk_count
    count = len(slots)
    vmem = pl.BlockSpec(memory_space=pltpu.VMEM)
    return pl.pallas_call(
        functools.partial(exchange_kernel, depth_count, blk_count, slots),
        out_shape=[jax.ShapeDtypeStruct((devices,) + x.shape[1:], x.dtype) for x in operands],
        in_specs=[vmem] * count,
        out_specs=[vmem] * count,
        scratch_shapes=[
            pltpu.SemaphoreType.DMA((count, devices)),
            pltpu.SemaphoreType.DMA((count, devices)),
            pltpu.SemaphoreType.DMA((count,)),
        ],
        compiler_params=pltpu.CompilerParams(collective_id=collective_id, has_side_effects=True),
    )(*operands)


def sections(jacobian, parts):
    rows, states = jacobian.shape
    width = states // parts
    return jacobian.reshape(rows, parts, width // LANES, LANES).transpose(1, 0, 2, 3)


def shards(jacobian, gain_inverse, variance):
    rows = jacobian.shape[0]
    depth_count = lax.axis_size("depth")
    blk_count = lax.axis_size("blk")
    devices = depth_count * blk_count
    left, right = exchange(
        ("depth", "blk"), 0, sections(jacobian, depth_count), sections(jacobian, blk_count)
    )
    left = left.reshape(devices * rows, -1)
    panel = right.reshape(devices * rows, -1)
    projected = jnp.dot(left, gain_inverse, preferred_element_type=jnp.float32)
    partial_sum = jnp.sum(projected * panel.astype(jnp.float32), axis=1)
    padded = jnp.pad(
        partial_sum.reshape(devices, 1, rows), ((0, 0), (0, SUBLANES - 1), (0, LANES - rows))
    )
    (gathered,) = exchange(("all",), 1, padded)
    quadratic = jnp.sum(gathered[:, 0, :rows], axis=0)
    return variance - quadratic


def solution(mesh):
    in_specs = (P(("depth", "blk"), None), P("depth", "blk"), P(("depth", "blk")))
    out_specs = P(("depth", "blk"))
    return jax.shard_map(shards, mesh=mesh, in_specs=in_specs, out_specs=out_specs, check_vma=False)
```

time: 96.4 us -> 61.8 us (0.64)
  blocking collectives: 70.1 us -> 0 us
  Pallas kernels: 0 us -> 46.9 us
  starting transfers between devices: 10.6 us -> 0 us
  local copies, waits for them, and re-layouts: 5.19 us -> 2.98 us
  other arithmetic: 0.68 us -> 2.53 us
    pallas_call x0 -> x2, Pallas kernels: none -> 46.9 us  [exchange(): pl.pallas_call(functools.partial(exchange_kernel, depth_count, blk_count,...]
    all_gather x2 -> x0, blocking collectives: 46.2 us -> none  [the longest x1 37.9 us: shards(): lax.all_gather(quarter_rows, 'blk', axis=0, tiled=True)]
    unnamed x2 -> x0, blocking collectives: 24 us -> none
    all_to_all x2 -> x0, starting transfers between devices: 10.6 us -> none  [the longest x1 6.31 us: shards(): lax.all_to_all(whole_rows, 'blk', split_axis=1, concat_axis=0, tiled=True)]
    unnamed x6 -> x3, local copies, waits for them, and re-layouts: 2.82 us -> 0.94 us
    all_to_all x2 -> x0, local copies, waits for them, and re-layouts: 1.55 us -> none  [shards(): lax.all_to_all(whole_rows, 'blk', split_axis=1, concat_axis=0, tiled=True)]
    unnamed x0 -> x1, other arithmetic: none -> 1.06 us
  transfers between devices with their start and end apart: 2 -> 0, of which waited for: 0 -> 0; matrix products, arithmetic and copies ran while one was open for 4% -> 0% of each run, Pallas kernels for 0% -> 0%
where the time goes in v1:
time: 61.8 us; the launch traced here: 61.5 us
  Pallas kernels  46.9 us (76%)
  matrix products  9.1 us (15%)
  local copies, waits for them, and re-layouts  2.98 us (5%)
  other arithmetic  2.53 us (4%)
    pallas_call x2, Pallas kernels, exchange(): pl.pallas_call(functools.partial(exchange_kernel, depth_count, blk_count,...  46.9 us
    dot_general x1, matrix products, shards(): projected = jnp.dot(left, gain_inverse, preferred_element_type=jnp.float32)  9.1 us
    reshape x2, local copies, waits for them, and re-layouts, sections(): jacobian.reshape(rows, parts, width // LANES, LANES).transpose(1, 0, 2, 3)  1.28 us

profile of v1, /device:TPU:0, one launch (start us, length us, event | category | flops | bytes accessed | tf_op | source)
XLA Modules:
  0.0 61.5 jit_solution(2897210296628969804)
XLA Ops:
  0.0 0.0 copy-start
  0.0 0.9 %copy.8 = bf16[1,3,128,128]{3,2,1,0:T(8,128)(2,1)S(1)} copy(bf16[1,3,128,128]{3,1,2,0:T(4,128)(2,1)} %bitcast.30) | data formatting | bytes 196608
  0.9 0.6 %copy.19 = bf16[3,8,16,128]{3,2,0,1:T(8,128)(2,1)} copy(bf16[3,8,16,128]{3,2,1,0:T(8,128)(2,1)S(1)} %bitcast.25) | data formatting | bytes 196608 | tf_op jit(solution)/shard_map/reshape | solution.py:97
  1.6 0.6 %copy.20 = bf16[3,4,32,128]{3,2,0,1:T(8,128)(2,1)} copy(bf16[3,4,32,128]{3,2,1,0:T(8,128)(2,1)S(1)} %bitcast.26) | data formatting | bytes 196608 | tf_op jit(solution)/shard_map/reshape | solution.py:97
  2.2 34.9 %shard_map.37 = (bf16[32,3,32,128]{3,2,1,0:T(8,128)(2,1)}, bf16[32,3,16,128]{3,2,1,0:T(8,128)(2,1)}) custom-call(bf16[4,3,32,128]{3,2,1,0:T(8,128)(2,1)} %bitcast.28, bf16[8,3,16,128]{3,2,1,0:T(8,128)(2,1)} %bitcast.27), custom_call_target="tpu_custom_call" | custom-call | tf_op jit(solution)/shard_map/pallas_call | solution.py:80
  37.1 1.1 %convert.1 = f32[12,8,16,128]{3,2,1,0:T(8,128)S(1)} convert(bf16[12,8,16,128]{3,2,1,0:T(8,128)(2,1)} %bitcast.29) | non-fusion elementwise | flops 196608 | bytes 1179648
  38.2 9.1 %fusion = f32[96]{0:T(128)S(1)} fusion(bf16[4096,2048]{1,0:T(8,128)(2,1)} %param.4, f32[12,8,16,128]{3,2,1,0:T(8,128)S(1)} %convert.1, bf16[12,8,32,128]{3,2,1,0:T(8,128)(2,1)} %bitcast.24), kind=kOutput, calls=%fused_computation.1 | convolution fusion | flops 1611005824 | bytes 18350464 | tf_op jit(solution)/shard_map/dot_general | solution.py:110
  47.3 0.1 reshape.18
  47.4 0.7 %pad.4.refs_0_ = f32[32,8,128]{2,1,0:T(8,128)} pad(f32[32,1,3]{2,1,0:T(1,128)S(1)} %bitcast.31, f32[]{:T(128)} %constant.1.clone.1), padding=0_0x0_7x0_125 | pad | bytes 131460 | tf_op jit(solution)/shard_map/jit(_pad)/pad | solution.py:112
  48.0 12.0 %shard_map.38 = f32[32,8,128]{2,1,0:T(8,128)} custom-call(f32[32,8,128]{2,1,0:T(8,128)} %pad.4.refs_0_), custom_call_target="tpu_custom_call" | custom-call | tf_op jit(solution)/shard_map/pallas_call | solution.py:80
  60.0 1.0 %slice_reduce_fusion = f32[3]{0:T(128)S(1)} fusion(f32[32,8,128]{2,1,0:T(8,128)} %shard_map.38), kind=kLoop, calls=%fused_computation.6 | loop fusion | flops 93 | bytes 396 | tf_op jit(solution)/shard_map/reduce_sum | solution.py:116
  61.0 0.0 copy-done
  61.0 0.5 sub.3
Async XLA Ops:
  0.0 61.0 %copy-start = (f32[3]{0:T(128)S(1)}, f32[3]{0:T(128)}, u32[]{:S(2)}) copy-start(f32[3]{0:T(128)} %param.5) | copy-start | bytes 40
